TPU v7x, 32 devices: a whole 2x2x4 slice. The times are simulated.
32 devices in a mesh: seq: 8 (over z, y), grp: 4 (over x, core).
Axes of the slice: x: 2, y: 2, z: 4, core: 2. Of those that a mesh axis runs over, the one named last changes fastest.
Arguments:
- query_nope: bfloat16 [4, 2, 128, 128], P(None, None, 'seq'), may hold values from -12.859821 to 12.859821
- query_rope: bfloat16 [4, 2, 128, 64], P(None, None, 'seq'), may hold values from -150 to 150
- latent_cache: bfloat16 [4, 8192, 576], P(None, ('seq', 'grp')), may hold values from -5 to 5
- lengths: int32 [4], replicated, may hold values from 4096 to 8192
- key_weight: bfloat16 [128, 128, 512], P('seq'), may hold values from -0.5 to 0.5
- value_weight: bfloat16 [128, 512, 128], P('seq'), may hold values from -0.25 to 0.25
- output_weight: bfloat16 [16384, 7168], P('seq', 'grp'), may hold values from -0.0625 to 0.0625
Outputs:
- mixed: bfloat16 [4, 2, 7168], P(None, None, ('grp', 'seq'))
All inputs are finite; a program needn't handle non-finite values.
Results may differ from a plain program's by a relative error of at most 0.0095.
Values may be sent and summed in bfloat16 or wider, within the bound.
No kernel may reach another device: no remote copies, remote signals or barrier semaphores. Data moves between devices by JAX's collectives and lax.ppermute only.
A program may use at most 64 MiB of HBM per device.

v0:
```python
import jax
import jax.numpy as jnp
from jax import lax
from jax.sharding import PartitionSpec as P

NEGATIVE = -1e30


def joined(part, axis, combine):
    gathered = jax.tree.map(lambda a: lax.all_gather(a, axis), part)

    def take(source):
        return jax.tree.map(lambda a: lax.dynamic_index_in_dim(a, source, 0, False), gathered)

    return lax.fori_loop(
        1, lax.axis_size(axis), lambda source, state: combine(state, take(source)), take(0)
    )


def shard_partial(queries, cache_block, limits, offset, factor, latent_width):
    raw_score = (
        jnp.einsum("bqhd,bpd->bqhp", queries, cache_block, preferred_element_type=jnp.float32)
        * factor
    )
    places = offset + lax.broadcasted_iota(jnp.int32, (1, 1, cache_block.shape[1]), 2)
    visible = places < limits[:, :, None]
    scores = jnp.where(visible[:, :, None, :], raw_score, NEGATIVE)
    maxima = jnp.max(scores, axis=-1)
    powers = jnp.exp(scores - maxima[..., None])
    totals = jnp.sum(powers, axis=-1)
    weights = powers.astype(jnp.bfloat16)
    summed = jnp.einsum(
        "bqhp,bpd->bqhd",
        weights,
        cache_block[:, :, :latent_width],
        preferred_element_type=jnp.float32,
    )
    return (maxima, totals, (summed / totals[..., None]).astype(jnp.bfloat16))


def merge_sources(partials, maxima, totals):
    highest = jnp.max(maxima, axis=0)
    shares = totals * jnp.exp(maxima - highest[None])
    summed = jnp.sum(shares, axis=0)
    numerator = jnp.sum(shares[..., None] * partials.astype(jnp.float32), axis=0)
    return (highest, summed, numerator / summed[..., None])


def merge_tuple(received):
    return merge_sources(received[0], received[1], received[2])


def join_pairs(earlier, later):
    highest = jnp.maximum(earlier[0], later[0])
    left_share = earlier[1] * jnp.exp(earlier[0] - highest)
    right_share = later[1] * jnp.exp(later[0] - highest)
    summed = left_share + right_share
    blended = (left_share[..., None] * earlier[2] + right_share[..., None] * later[2]) / summed[
        ..., None
    ]
    return (highest, summed, blended)


def absorb(query_nope, query_rope, key_weight):
    absorbed = jnp.einsum(
        "bqhn,hnd->bqhd", query_nope, key_weight, preferred_element_type=jnp.float32
    )
    return jnp.concatenate([absorbed.astype(jnp.bfloat16), query_rope], axis=-1)


def up_project(latent_out, value_weight):
    values = jnp.einsum(
        "bqhd,hde->bqhe", latent_out, value_weight, preferred_element_type=jnp.float32
    ).astype(jnp.bfloat16)
    return values.reshape(values.shape[0], values.shape[1], values.shape[2] * values.shape[3])


def shards(query_nope, query_rope, latent_cache, lengths, key_weight, value_weight, output_weight):
    latent_width = key_weight.shape[2]
    factor = float(query_nope.shape[3] + query_rope.shape[3]) ** (-0.5)
    positions = latent_cache.shape[1]
    drafts = query_nope.shape[1]
    offset = (lax.axis_index("seq") * lax.axis_size("grp") + lax.axis_index("grp")) * positions
    limits = lengths[:, None] - drafts + 1 + lax.broadcasted_iota(jnp.int32, (1, drafts), 1)
    own_queries = absorb(query_nope, query_rope, key_weight)
    maxima, totals, partials = shard_partial(
        lax.all_gather(own_queries, "seq", axis=2, tiled=True),
        latent_cache,
        limits,
        offset,
        factor,
        latent_width,
    )
    partials, maxima, totals = (partials, maxima, totals)
    sources = (partials[None], maxima[None], totals[None])
    gathered = merge_tuple(
        (
            lax.all_to_all(
                sources[0].astype(jnp.float32), "seq", split_axis=3, concat_axis=0, tiled=True
            ).astype(jnp.bfloat16),
            lax.all_to_all(sources[1], "seq", split_axis=3, concat_axis=0, tiled=True),
            lax.all_to_all(sources[2], "seq", split_axis=3, concat_axis=0, tiled=True),
        )
    )
    highest, summed, blended = joined((gathered[0], gathered[1], gathered[2]), "grp", join_pairs)
    values = up_project(blended.astype(jnp.bfloat16), value_weight)
    head_terms = jnp.dot(values, output_weight, preferred_element_type=jnp.float32)
    reduced = lax.psum_scatter(head_terms, "seq", scatter_dimension=2, tiled=True)
    return reduced.astype(jnp.bfloat16)


def solution(mesh):
    in_specs = (
        P(None, None, "seq", None),
        P(None, None, "seq", None),
        P(None, ("seq", "grp"), None),
        P(),
        P("seq", None, None),
        P("seq", None, None),
        P("seq", "grp"),
    )
    out_specs = P(None, None, ("grp", "seq"))
    return jax.shard_map(shards, mesh=mesh, in_specs=in_specs, out_specs=out_specs, check_vma=False)
```

profile of v0, /device:TPU:0, one launch (start us, length us, event | category | flops | bytes accessed | tf_op | source)
XLA Modules:
  0.0 212.3 jit_solution(17703678175560071938)
XLA Ops:
  6.5 0.9 copy.29
  8.1 1.1 fusion.18
  10.2 44.5 %all-gather.5.cloned.1.call-done = bf16[4,2,128,576]{3,0,1,2:T(4,128)(2,1)} async-done(((bf16[4,2,16,576]{3,0,1,2:T(4,128)(2,1)}), bf16[4,2,128,576]{3,0,1,2:T(4,128)(2,1)}) %all-gather.5.cloned.1.call-update) | async-done | bytes 1179664 | tf_op jit(solution)/shard_map/all_gather | solution.py:87
  54.7 2.4 %fusion.42 = (f32[4,2,128]{2,1,0:T(2,128)S(1)}, f32[4,2,128,256]{3,2,1,0:T(8,128)S(1)}) fusion(bf16[4,256,576]{1,2,0:T(8,128)(2,1)} %param.11, bf16[4,2,128,576]{3,0,1,2:T(4,128)(2,1)} %all-gather.5.cloned.1.call-done, pred[4,2,256]{2,1,0:T(4,128)(4,1)S(1)} %broadcast_compare_fusion), kind=kOutput, calls=%fused_computation.50 | convolution fusion | flops 302775296 | bytes 3414016 | tf_op jit(solution)/shard_map/bqhd,bpd->bqhp/dot_general | solution.py:22
  57.7 0.8 reshape.85
  58.5 3.4 %all-to-all-start.1 = ((f32[8,1,128]{2,1,0:T(1,128)}), f32[8,1,128]{2,1,0:T(1,128)S(1)}, u32[]{:S(2)}, u32[]{:S(2)}) async-start(f32[8,1,128]{2,1,0:T(1,128)} %reshape.85), calls=%async_computation.1 | async-start | bytes 8192 | tf_op jit(solution)/shard_map/all_to_all | solution.py:102
  62.9 5.5 %all-to-all-done.1 = f32[8,1,128]{2,1,0:T(1,128)S(1)} async-done(((f32[8,1,128]{2,1,0:T(1,128)}), f32[8,1,128]{2,1,0:T(1,128)S(1)}, u32[]{:S(2)}, u32[]{:S(2)}) %all-to-all-start.1) | async-done | bytes 4128 | tf_op jit(solution)/shard_map/all_to_all | solution.py:102
  68.4 3.3 %all-to-all-start = ((f32[8,1,128]{2,1,0:T(1,128)}), f32[8,1,128]{2,1,0:T(1,128)S(1)}, u32[]{:S(2)}, u32[]{:S(2)}) async-start(f32[8,1,128]{2,1,0:T(1,128)} %reshape.83), calls=%async_computation | async-start | bytes 8192 | tf_op jit(solution)/shard_map/all_to_all | solution.py:101
  71.7 1.7 fusion.11
  73.5 2.1 copy.38
  75.6 2.5 %all-to-all-done = f32[8,1,128]{2,1,0:T(1,128)S(1)} async-done(((f32[8,1,128]{2,1,0:T(1,128)}), f32[8,1,128]{2,1,0:T(1,128)S(1)}, u32[]{:S(2)}, u32[]{:S(2)}) %all-to-all-start) | async-done | bytes 4128 | tf_op jit(solution)/shard_map/all_to_all | solution.py:101
  78.1 3.6 %all-to-all-start.2 = ((bf16[1,4,2,128,512]{4,2,1,0,3:T(2,128)(2,1)}), bf16[1,4,2,128,512]{4,2,1,0,3:T(2,128)(2,1)S(1)}, u32[]{:S(2)}, u32[]{:S(2)}) async-start(bf16[1,4,2,128,512]{4,2,1,0,3:T(2,128)(2,1)} %copy.38), calls=%async_computation.2 | async-start | bytes 2097152 | tf_op jit(solution)/shard_map/all_to_all | solution.py:98
  83.1 1.6 copy.35
  85.6 0.9 copy.32
  86.6 1.8 fusion.40
  88.4 16.5 %all-to-all-done.2 = bf16[1,4,2,128,512]{4,2,1,0,3:T(2,128)(2,1)S(1)} async-done(((bf16[1,4,2,128,512]{4,2,1,0,3:T(2,128)(2,1)}), bf16[1,4,2,128,512]{4,2,1,0,3:T(2,128)(2,1)S(1)}, u32[]{:S(2)}, u32[]{:S(2)}) %all-to-all-start.2) | async-done | bytes 1048608 | tf_op jit(solution)/shard_map/all_to_all | solution.py:98
  104.9 2.3 %fusion.7 = f32[4,2,16,512]{3,1,0,2:T(2,128)S(1)} fusion(bf16[1,4,2,8,16,512]{5,2,1,4,3,0:T(2,128)(2,1)S(1)} %bitcast.108, f32[8,4,2,16]{2,1,3,0:T(4,128)} %get-tuple-element.201), kind=kLoop, calls=%fused_computation.13 | loop fusion | flops 1507328 | bytes 1314816 | tf_op jit(solution)/shard_map/reduce_sum | solution.py:45
  107.3 0.9 copy.39
  108.5 5.2 %all-gather.1 = f32[16,2,16]{2,1,0:T(2,128)S(1)} all-gather(f32[4,2,16]{2,1,0:T(2,128)S(1)} %copy.36), channel_id=3, replica_groups=mesh['seq'=8,'grp'=4] {'grp'}, dimensions={0}, use_global_device_ids=true | all-gather | bytes 2560 | tf_op jit(solution)/shard_map/all_gather | solution.py:10
  113.7 5.2 %all-gather = f32[16,2,16]{2,1,0:T(2,128)S(1)} all-gather(f32[4,2,16]{2,1,0:T(2,128)S(1)} %copy.33), channel_id=2, replica_groups=mesh['seq'=8,'grp'=4] {'grp'}, dimensions={0}, use_global_device_ids=true | all-gather | bytes 2560 | tf_op jit(solution)/shard_map/all_gather | solution.py:10
  118.9 5.1 %all-gather.7.cloned.1.call-done = f32[4,4,2,16,512]{4,3,2,1,0:T(8,128)} async-done(((f32[1,4,2,16,512]{4,3,2,1,0:T(8,128)}), f32[4,4,2,16,512]{4,3,2,1,0:T(8,128)}) %all-gather.7.cloned.1.call-update) | async-done | bytes 1048592 | tf_op jit(solution)/shard_map/all_gather | solution.py:10
  124.0 1.0 slice_bitcast_fusion
  124.9 3.5 %while.19 = (s32[]{:T(128)}, f32[4,2,16]{2,1,0:T(2,128)S(1)}, f32[4,2,16]{2,1,0:T(2,128)S(1)}, f32[4,2,16,512]{3,2,1,0:T(8,128)S(1)}, f32[4,4,2,16]{3,2,1,0:T(2,...) while((s32[]{:T(128)}, f32[4,2,16]{2,1,0:T(2,128)S(1)}, ...), condition=%wide.region_6.7_spmd, body=%wide.region_5.6_spmd.sunk | while | flops 262917 | bytes 792207 | solution.py:15
  125.0 1.1 fusion.46
  126.2 1.1 fusion.46
  127.3 1.1 fusion.46
  128.4 2.0 fusion.24
  130.5 4.2 %fusion.3 = f32[4,2,1792]{2,0,1:T(4,128)S(1)} fusion(bf16[2048,1792]{1,0:T(8,128)(2,1)} %param.15, bf16[16,2,1,4,128]{4,3,2,1,0:T(4,128)(2,1)S(1)} %fusion.24), kind=kOutput, calls=%fused_computation.8 | convolution fusion | flops 58720256 | bytes 7430144 | tf_op jit(solution)/shard_map/dot_general | solution.py:107
  134.7 2.3 %copy.49 = f32[4,2,1792]{0,1,2:T(2,128)} copy(f32[4,2,1792]{2,0,1:T(4,128)S(1)} %fusion.3) | data formatting | bytes 114688
  137.0 3.1 %reshape.81 = f32[1792,8]{1,0:T(8,128)} reshape(f32[1792,2,4]{2,1,0:T(2,128)} %bitcast.107) | data formatting | bytes 114688
  140.1 63.9 %reduce-scatter.4.cloned.1.call-done = f32[224,8]{1,0:T(8,128)} async-done(((f32[1792,8]{1,0:T(8,128)}), f32[224,8]{1,0:T(8,128)}) %reduce-scatter.4.cloned.1.call-update) | async-done | bytes 7184
  204.0 1.0 reshape.82
  (36 shorter events, 6.8 us)
Async XLA Ops:
  6.5 1.6 copy-start
  6.5 3.5 %copy-start.1 = (s32[4]{0:T(128)S(1)}, s32[4]{0:T(128)}, u32[]{:S(2)}) copy-start(s32[4]{0:T(128)} %param.12) | copy-start | bytes 52
  6.5 48.2 %all-gather.5.cloned.1.call-start = ((), (), s32[]{:S(2)}) async-start(), calls=%async_computation.4 | async-start | bytes 1474560 | tf_op jit(solution)/shard_map/all_gather | solution.py:87
  58.5 9.9 %all-to-all-start.1 = ((f32[8,1,128]{2,1,0:T(1,128)}), f32[8,1,128]{2,1,0:T(1,128)S(1)}, u32[]{:S(2)}, u32[]{:S(2)}) async-start(f32[8,1,128]{2,1,0:T(1,128)} %reshape.85), calls=%async_computation.1 | async-start | bytes 8192 | tf_op jit(solution)/shard_map/all_to_all | solution.py:102
  68.4 9.7 %all-to-all-start = ((f32[8,1,128]{2,1,0:T(1,128)}), f32[8,1,128]{2,1,0:T(1,128)S(1)}, u32[]{:S(2)}, u32[]{:S(2)}) async-start(f32[8,1,128]{2,1,0:T(1,128)} %reshape.83), calls=%async_computation | async-start | bytes 8192 | tf_op jit(solution)/shard_map/all_to_all | solution.py:101
  78.1 26.8 %all-to-all-start.2 = ((bf16[1,4,2,128,512]{4,2,1,0,3:T(2,128)(2,1)}), bf16[1,4,2,128,512]{4,2,1,0,3:T(2,128)(2,1)S(1)}, u32[]{:S(2)}, u32[]{:S(2)}) async-start(bf16[1,4,2,128,512]{4,2,1,0,3:T(2,128)(2,1)} %copy.38), calls=%async_computation.2 | async-start | bytes 2097152 | tf_op jit(solution)/shard_map/all_to_all | solution.py:98
  81.6 42.3 %all-gather.7.cloned.1.call-start = ((), (), s32[]{:S(2)}) async-start(), calls=%async_computation.5 | async-start | bytes 1310720 | tf_op jit(solution)/shard_map/all_gather | solution.py:10
  108.2 95.8 %reduce-scatter.4.cloned.1.call-start = ((), (), s32[]{:S(2)}) async-start(), calls=%async_computation.6 | async-start | bytes 1032192
Sparse Core Ops, SparseCore 0:
  10.2 44.5 all-gather.4
  108.4 15.5 all-gather.6
  140.3 63.6 reduce-scatter.3
where the time goes:
time: 213 us; the launch traced here: 212 us
  waiting for transfers between devices  138 us (65%)
  local copies, waits for them, and re-layouts  18.2 us (9%)
  between operations  13.3 us (6%)
  matrix products  11.5 us (5%)
  starting transfers between devices  10.4 us (5%)
  blocking collectives  10.4 us (5%)
  other arithmetic  10.3 us (5%)
    unnamed x4, waiting for transfers between devices  63.9 us
    all_gather x1, waiting for transfers between devices, shards(): lax.all_gather(own_queries, 'seq', axis=2, tiled=True)  44.5 us
    all_to_all x1, waiting for transfers between devices, shards(): lax.all_to_all(sources[0].astype(jnp.float32), 'seq', split_axis=3, conca...  16.5 us
    all_gather x2, blocking collectives, joined(): gathered = jax.tree.map(lambda a: lax.all_gather(a, axis), part)  10.4 us
    unnamed x13, local copies, waits for them, and re-layouts  10.2 us
    all_to_all x1, waiting for transfers between devices, shards(): lax.all_to_all(sources[2], 'seq', split_axis=3, concat_axis=0, tiled=True)  5.53 us
    all_gather x1, waiting for transfers between devices, joined(): gathered = jax.tree.map(lambda a: lax.all_gather(a, axis), part)  5.1 us
  transfers between devices with their start and end apart: 6, of which 6 were waited for; matrix products, arithmetic and copies ran while one was open for 6% of the time, Pallas kernels for 0%

commit v1 on v0

--- a/solution.py
+++ b/solution.py
@@ -4,6 +4,30 @@
 from jax.sharding import PartitionSpec as P
 
 NEGATIVE = -1e30
+
+
+def in_blocks(x, dim, size):
+    lengths = x.shape
+    blocks = x.reshape(*lengths[:dim], size, lengths[dim] // size, *lengths[dim + 1 :])
+    return jnp.moveaxis(blocks, dim, 0)
+
+
+def in_order(blocks, dim):
+    shape = list(blocks.shape[1:])
+    shape[dim] *= blocks.shape[0]
+    return jnp.moveaxis(blocks, 0, dim).reshape(shape)
+
+
+def exchange_directly(array, axis, split_dim, concat_dim):
+    size, here = (lax.axis_size(axis), lax.axis_index(axis))
+    pieces = in_blocks(array, split_dim, size)
+    out = pieces
+    for step in range(1, size):
+        target, source = ((here + step) % size, (here - step) % size)
+        sent = lax.dynamic_index_in_dim(pieces, target, 0)
+        other = lax.ppermute(sent, axis, [(i, (i + step) % size) for i in range(size)])
+        out = lax.dynamic_update_slice_in_dim(out, other, source, axis=0)
+    return in_order(out, concat_dim)
 
 
 def joined(part, axis, combine):
@@ -95,9 +119,7 @@
     sources = (partials[None], maxima[None], totals[None])
     gathered = merge_tuple(
         (
-            lax.all_to_all(
-                sources[0].astype(jnp.float32), "seq", split_axis=3, concat_axis=0, tiled=True
-            ).astype(jnp.bfloat16),
+            exchange_directly(sources[0].astype(jnp.float32), "seq", 3, 0).astype(jnp.bfloat16),
             lax.all_to_all(sources[1], "seq", split_axis=3, concat_axis=0, tiled=True),
             lax.all_to_all(sources[2], "seq", split_axis=3, concat_axis=0, tiled=True),
         )

time: 213 us -> 207 us (0.972)
  waiting for transfers between devices: 138 us -> 119 us
  starting transfers between devices: 10.4 us -> 19.4 us
  local copies, waits for them, and re-layouts: 18.2 us -> 22.9 us
    all_to_all x1 -> x0, waiting for transfers between devices: 16.5 us -> none  [shards(): lax.all_to_all(sources[0].astype(jnp.float32), 'seq', split_axis=3, conca...]
    ppermute x0 -> x7, starting transfers between devices: none -> 12.6 us  [exchange_directly(): lax.ppermute(sent, axis, [(i, (i + step) % size) for i in range(size)])]
    dynamic_update_slice x0 -> x7, local copies, waits for them, and re-layouts: none -> 4.62 us  [exchange_directly(): out = lax.dynamic_update_slice_in_dim(out, other, source, axis=0)]
    all_to_all x1 -> x0, starting transfers between devices: 3.56 us -> none  [shards(): lax.all_to_all(sources[0].astype(jnp.float32), 'seq', split_axis=3, conca...]
    all_to_all x1, waiting for transfers between devices: 2.53 us -> 0.01 us  [shards(): lax.all_to_all(sources[1], 'seq', split_axis=3, concat_axis=0, tiled=True)]
    unnamed x13 -> x15, local copies, waits for them, and re-layouts: 10.2 us -> 11.2 us
  transfers between devices with their start and end apart: 6 -> 12, of which waited for: 6 -> 4; matrix products, arithmetic and copies ran while one was open for 6% -> 8% of each run, Pallas kernels for 0% -> 0%
where the time goes in v1:
time: 207 us; the launch traced here: 206 us
  waiting for transfers between devices  119 us (57%)
  local copies, waits for them, and re-layouts  22.9 us (11%)
  starting transfers between devices  19.4 us (9%)
  between operations  13.6 us (7%)
  matrix products  11.8 us (6%)
  blocking collectives  10.4 us (5%)
  other arithmetic  8.73 us (4%)
    unnamed x4, waiting for transfers between devices  63.9 us
    all_gather x1, waiting for transfers between devices, shards(): lax.all_gather(own_queries, 'seq', axis=2, tiled=True)  44.3 us
    ppermute x7, starting transfers between devices, exchange_directly(): lax.ppermute(sent, axis, [(i, (i + step) % size) for i in range(size)])  12.6 us
    unnamed x15, local copies, waits for them, and re-layouts  11.2 us
    all_gather x2, blocking collectives, joined(): gathered = jax.tree.map(lambda a: lax.all_gather(a, axis), part)  10.4 us
    all_gather x1, waiting for transfers between devices, joined(): gathered = jax.tree.map(lambda a: lax.all_gather(a, axis), part)  7.17 us
    dynamic_update_slice x7, local copies, waits for them, and re-layouts, exchange_directly(): out = lax.dynamic_update_slice_in_dim(out, other, source, axis=0)  4.62 us
    dot_general x1, matrix products, shards(): jnp.dot(values, output_weight, preferred_element_type=jnp.float32)  4.22 us
  transfers between devices with their start and end apart: 12, of which 4 were waited for; matrix products, arithmetic and copies ran while one was open for 8% of the time, Pallas kernels for 0%

profile of v1, /device:TPU:0, one launch (start us, length us, event | category | flops | bytes accessed | tf_op | source)
XLA Modules:
  0.0 205.8 jit_solution(10166744433918149020)
XLA Ops:
  8.1 1.1 fusion.15
  10.5 44.3 %all-gather.5.cloned.1.call-done = bf16[4,2,128,576]{3,0,1,2:T(4,128)(2,1)} async-done(((bf16[4,2,16,576]{3,0,1,2:T(4,128)(2,1)}), bf16[4,2,128,576]{3,0,1,2:T(4,128)(2,1)}) %all-gather.5.cloned.1.call-update) | async-done | bytes 1179664 | tf_op jit(solution)/shard_map/all_gather | solution.py:111
  54.8 2.4 %fusion.39 = (f32[4,2,128]{2,1,0:T(2,128)S(1)}, f32[4,2,128,256]{3,2,1,0:T(8,128)S(1)}) fusion(bf16[4,256,576]{1,2,0:T(8,128)(2,1)} %param.11, bf16[4,2,128,576]{3,0,1,2:T(4,128)(2,1)} %all-gather.5.cloned.1.call-done, pred[4,2,256]{2,1,0:T(4,128)(4,1)S(1)} %broadcast_compare_fusion), kind=kOutput, calls=%fused_computation.62 | convolution fusion | flops 302775296 | bytes 3414016 | tf_op jit(solution)/shard_map/bqhd,bpd->bqhp/dot_general | solution.py:46
  57.1 1.0 copy-done.1
  59.5 3.4 %all-to-all-start.1 = ((f32[8,1,128]{2,1,0:T(1,128)}), f32[8,1,128]{2,1,0:T(1,128)S(1)}, u32[]{:S(2)}, u32[]{:S(2)}) async-start(f32[8,1,128]{2,1,0:T(1,128)} %reshape.132), calls=%async_computation.1 | async-start | bytes 8192 | tf_op jit(solution)/shard_map/all_to_all | solution.py:124
  62.9 2.0 divide_convert_fusion
  65.9 3.5 %all-to-all-done.1 = f32[8,1,128]{2,1,0:T(1,128)S(1)} async-done(((f32[8,1,128]{2,1,0:T(1,128)}), f32[8,1,128]{2,1,0:T(1,128)S(1)}, u32[]{:S(2)}, u32[]{:S(2)}) %all-to-all-start.1) | async-done | bytes 4128 | tf_op jit(solution)/shard_map/all_to_all | solution.py:124
  69.4 3.3 %all-to-all-start = ((f32[8,1,128]{2,1,0:T(1,128)}), f32[8,1,128]{2,1,0:T(1,128)S(1)}, u32[]{:S(2)}, u32[]{:S(2)}) async-start(f32[8,1,128]{2,1,0:T(1,128)} %reshape.130), calls=%async_computation | async-start | bytes 8192 | tf_op jit(solution)/shard_map/all_to_all | solution.py:123
  73.7 1.9 collective-permute-start
  75.6 1.5 collective-permute-start.1
  77.1 2.4 %collective-permute-start.2 = (bf16[1,1,4,2,16,512]{5,4,3,2,1,0:T(8,128)(2,1)}, bf16[1,1,4,2,16,512]{5,4,3,2,1,0:T(8,128)(2,1)}, u32[]{:S(2)}, u32[]{:S(2)}) collective-permute-start(bf16[1,1,4,2,16,512]{5,4,3,2,1,0:T(8,128)(2,1)} %get-tuple-element.205), channel_id=1, source_target_pairs={{0,12},{4,16},{8,20},{12,24},{16,28},{20,0},{24,4},{28,8},{1,13},{... | collective-permute-start | bytes 393224 | tf_op jit(solution)/shard_map/ppermute | solution.py:28
  79.4 1.4 collective-permute-start.3
  80.9 2.4 %collective-permute-start.4 = (bf16[1,1,4,2,16,512]{5,4,3,2,1,0:T(8,128)(2,1)}, bf16[1,1,4,2,16,512]{5,4,3,2,1,0:T(8,128)(2,1)}, u32[]{:S(2)}, u32[]{:S(2)}) collective-permute-start(bf16[1,1,4,2,16,512]{5,4,3,2,1,0:T(8,128)(2,1)} %get-tuple-element.203), channel_id=1, source_target_pairs={{0,20},{4,24},{8,28},{12,0},{16,4},{20,8},{24,12},{28,16},{1,21},{... | collective-permute-start | bytes 393224 | tf_op jit(solution)/shard_map/ppermute | solution.py:28
  84.5 1.6 copy.35
  87.9 1.8 fusion.37
  89.6 1.2 copy.37
  90.9 1.5 collective-permute-start.5
  93.4 1.5 collective-permute-start.6
  99.9 5.2 %all-gather.1 = f32[16,2,16]{2,1,0:T(2,128)S(1)} all-gather(f32[4,2,16]{2,1,0:T(2,128)S(1)} %copy.36), channel_id=3, replica_groups=mesh['seq'=8,'grp'=4] {'grp'}, dimensions={0}, use_global_device_ids=true | all-gather | bytes 2560 | tf_op jit(solution)/shard_map/all_gather | solution.py:34
  105.1 5.2 %all-gather = f32[16,2,16]{2,1,0:T(2,128)S(1)} all-gather(f32[4,2,16]{2,1,0:T(2,128)S(1)} %copy.33), channel_id=2, replica_groups=mesh['seq'=8,'grp'=4] {'grp'}, dimensions={0}, use_global_device_ids=true | all-gather | bytes 2560 | tf_op jit(solution)/shard_map/all_gather | solution.py:34
  110.3 7.2 %all-gather.7.cloned.1.call-done = f32[4,4,2,16,512]{4,3,2,1,0:T(8,128)} async-done(((f32[1,4,2,16,512]{4,3,2,1,0:T(8,128)}), f32[4,4,2,16,512]{4,3,2,1,0:T(8,128)}) %all-gather.7.cloned.1.call-update) | async-done | bytes 1048592 | tf_op jit(solution)/shard_map/all_gather | solution.py:34
  117.5 1.0 slice_bitcast_fusion
  118.4 3.5 %while.19 = (s32[]{:T(128)}, f32[4,2,16]{2,1,0:T(2,128)S(1)}, f32[4,2,16]{2,1,0:T(2,128)S(1)}, f32[4,2,16,512]{3,2,1,0:T(8,128)S(1)}, f32[4,4,2,16]{3,2,1,0:T(2,...) while((s32[]{:T(128)}, f32[4,2,16]{2,1,0:T(2,128)S(1)}, ...), condition=%wide.region_6.7_spmd, body=%wide.region_5.6_spmd.sunk | while | flops 262917 | bytes 792215 | solution.py:39
  118.5 1.1 fusion.43
  119.6 1.1 fusion.43
  120.8 1.1 fusion.43
  121.9 2.0 fusion.21
  124.0 4.2 %fusion.3 = f32[4,2,1792]{2,0,1:T(4,128)S(1)} fusion(bf16[2048,1792]{1,0:T(8,128)(2,1)} %param.15, bf16[16,2,1,4,128]{4,3,2,1,0:T(4,128)(2,1)S(1)} %fusion.21), kind=kOutput, calls=%fused_computation.8 | convolution fusion | flops 58720256 | bytes 7430144 | tf_op jit(solution)/shard_map/dot_general | solution.py:129
  128.2 2.3 %copy.49 = f32[4,2,1792]{0,1,2:T(2,128)} copy(f32[4,2,1792]{2,0,1:T(4,128)S(1)} %fusion.3) | data formatting | bytes 114688
  130.5 3.1 %reshape.128 = f32[1792,8]{1,0:T(8,128)} reshape(f32[1792,2,4]{2,1,0:T(2,128)} %bitcast.129) | data formatting | bytes 114688
  133.6 63.9 %reduce-scatter.4.cloned.1.call-done = f32[224,8]{1,0:T(8,128)} async-done(((f32[1792,8]{1,0:T(8,128)}), f32[224,8]{1,0:T(8,128)}) %reduce-scatter.4.cloned.1.call-update) | async-done | bytes 7184
  197.5 1.0 reshape.129
  (57 shorter events, 15.7 us)
Async XLA Ops:
  6.5 1.6 copy-start
  6.5 3.8 %copy-start.2 = (s32[4]{0:T(128)S(1)}, s32[4]{0:T(128)}, u32[]{:S(2)}) copy-start(s32[4]{0:T(128)} %param.12) | copy-start | bytes 52
  6.5 48.2 %all-gather.5.cloned.1.call-start = ((), (), s32[]{:S(2)}) async-start(), calls=%async_computation.3 | async-start | bytes 1474560 | tf_op jit(solution)/shard_map/all_gather | solution.py:111
  57.1 1.0 copy-start.1
  59.5 9.9 %all-to-all-start.1 = ((f32[8,1,128]{2,1,0:T(1,128)}), f32[8,1,128]{2,1,0:T(1,128)S(1)}, u32[]{:S(2)}, u32[]{:S(2)}) async-start(f32[8,1,128]{2,1,0:T(1,128)} %reshape.132), calls=%async_computation.1 | async-start | bytes 8192 | tf_op jit(solution)/shard_map/all_to_all | solution.py:124
  69.4 16.7 %all-to-all-start = ((f32[8,1,128]{2,1,0:T(1,128)}), f32[8,1,128]{2,1,0:T(1,128)S(1)}, u32[]{:S(2)}, u32[]{:S(2)}) async-start(f32[8,1,128]{2,1,0:T(1,128)} %reshape.130), calls=%async_computation | async-start | bytes 8192 | tf_op jit(solution)/shard_map/all_to_all | solution.py:123
  72.7 44.7 %all-gather.7.cloned.1.call-start = ((), (), s32[]{:S(2)}) async-start(), calls=%async_computation.4 | async-start | bytes 1310720 | tf_op jit(solution)/shard_map/all_gather | solution.py:34
  73.7 17.2 %collective-permute-start = (bf16[1,1,4,2,16,512]{5,4,3,2,1,0:T(8,128)(2,1)}, bf16[1,1,4,2,16,512]{5,4,3,2,1,0:T(8,128)(2,1)}, u32[]{:S(2)}, u32[]{:S(2)}) collective-permute-start(bf16[1,1,4,2,16,512]{5,4,3,2,1,0:T(8,128)(2,1)} %get-tuple-element.207), channel_id=1, source_target_pairs={{0,4},{4,8},{8,12},{12,16},{16,20},{20,24},{24,28},{28,0},{1,5},{5... | collective-permute-start | bytes 393224 | tf_op jit(solution)/shard_map/ppermute | solution.py:28
  75.6 17.8 %collective-permute-start.1 = (bf16[1,1,4,2,16,512]{5,4,3,2,1,0:T(8,128)(2,1)}, bf16[1,1,4,2,16,512]{5,4,3,2,1,0:T(8,128)(2,1)}, u32[]{:S(2)}, u32[]{:S(2)}) collective-permute-start(bf16[1,1,4,2,16,512]{5,4,3,2,1,0:T(8,128)(2,1)} %get-tuple-element.206), channel_id=1, source_target_pairs={{0,8},{4,12},{8,16},{12,20},{16,24},{20,28},{24,0},{28,4},{1,9},{5... | collective-permute-start | bytes 393224 | tf_op jit(solution)/shard_map/ppermute | solution.py:28
  77.1 18.7 %collective-permute-start.2 = (bf16[1,1,4,2,16,512]{5,4,3,2,1,0:T(8,128)(2,1)}, bf16[1,1,4,2,16,512]{5,4,3,2,1,0:T(8,128)(2,1)}, u32[]{:S(2)}, u32[]{:S(2)}) collective-permute-start(bf16[1,1,4,2,16,512]{5,4,3,2,1,0:T(8,128)(2,1)} %get-tuple-element.205), channel_id=1, source_target_pairs={{0,12},{4,16},{8,20},{12,24},{16,28},{20,0},{24,4},{28,8},{1,13},{... | collective-permute-start | bytes 393224 | tf_op jit(solution)/shard_map/ppermute | solution.py:28
  79.4 17.3 %collective-permute-start.3 = (bf16[1,1,4,2,16,512]{5,4,3,2,1,0:T(8,128)(2,1)}, bf16[1,1,4,2,16,512]{5,4,3,2,1,0:T(8,128)(2,1)}, u32[]{:S(2)}, u32[]{:S(2)}) collective-permute-start(bf16[1,1,4,2,16,512]{5,4,3,2,1,0:T(8,128)(2,1)} %get-tuple-element.204), channel_id=1, source_target_pairs={{0,16},{4,20},{8,24},{12,28},{16,0},{20,4},{24,8},{28,12},{1,17},{... | collective-permute-start | bytes 393224 | tf_op jit(solution)/shard_map/ppermute | solution.py:28
  80.9 16.8 %collective-permute-start.4 = (bf16[1,1,4,2,16,512]{5,4,3,2,1,0:T(8,128)(2,1)}, bf16[1,1,4,2,16,512]{5,4,3,2,1,0:T(8,128)(2,1)}, u32[]{:S(2)}, u32[]{:S(2)}) collective-permute-start(bf16[1,1,4,2,16,512]{5,4,3,2,1,0:T(8,128)(2,1)} %get-tuple-element.203), channel_id=1, source_target_pairs={{0,20},{4,24},{8,28},{12,0},{16,4},{20,8},{24,12},{28,16},{1,21},{... | collective-permute-start | bytes 393224 | tf_op jit(solution)/shard_map/ppermute | solution.py:28
  90.9 7.7 %collective-permute-start.5 = (bf16[1,1,4,2,16,512]{5,4,3,2,1,0:T(8,128)(2,1)}, bf16[1,1,4,2,16,512]{5,4,3,2,1,0:T(8,128)(2,1)S(1)}, u32[]{:S(2)}, u32[]{:S(2)}) collective-permute-start(bf16[1,1,4,2,16,512]{5,4,3,2,1,0:T(8,128)(2,1)} %get-tuple-element.208), channel_id=1, source_target_pairs={{0,24},{4,28},{8,0},{12,4},{16,8},{20,12},{24,16},{28,20},{1,25},{... | collective-permute-start | bytes 393224 | tf_op jit(solution)/shard_map/ppermute | solution.py:28
  93.4 5.3 %collective-permute-start.6 = (bf16[1,1,4,2,16,512]{5,4,3,2,1,0:T(8,128)(2,1)}, bf16[1,1,4,2,16,512]{5,4,3,2,1,0:T(8,128)(2,1)S(1)}, u32[]{:S(2)}, u32[]{:S(2)}) collective-permute-start(bf16[1,1,4,2,16,512]{5,4,3,2,1,0:T(8,128)(2,1)} %get-tuple-element.202), channel_id=1, source_target_pairs={{0,28},{4,0},{8,4},{12,8},{16,12},{20,16},{24,20},{28,24},{1,29},{... | collective-permute-start | bytes 393224 | tf_op jit(solution)/shard_map/ppermute | solution.py:28
  99.7 97.8 %reduce-scatter.4.cloned.1.call-start = ((), (), s32[]{:S(2)}) async-start(), calls=%async_computation.5 | async-start | bytes 1032192
Sparse Core Ops, SparseCore 0:
  10.2 44.5 all-gather.4
  99.9 17.5 all-gather.6
  133.7 63.7 reduce-scatter.3
